TPU v7x, 32 devices: a whole 2x2x4 slice. The times are simulated.
32 devices in a mesh: slab: 4 (over y, x), sta: 8 (over z, core).
Axes of the slice: x: 2, y: 2, z: 4, core: 2. Of those that a mesh axis runs over, the one named last changes fastest.
Arguments:
- station_place: float32 [32, 2], P('sta'), may hold values from 0 to 1
- station_height: float32 [32], P('sta'), may hold values from 2 to 8
- cell_weight: float32 [256, 256, 64], P('slab'), may hold values from 0.5 to 2
- kept: int32 [4, 32, 16], P('slab', 'sta'), may hold values from 0 to 8191, as said below
- dest: int32 [4, 32, 16, 1], P('slab', 'sta'), may hold values from 0 to 7; in each aligned block of 64 rows (0 to 63, 64 to 127, ..., all dimensions but the last counted through in order) at most 24 rows name the same one
Outputs:
- owned_blocks: float32 [4, 8, 8, 24, 128], P('slab', 'sta')
Inputs may be any that keep to these rules, and one draw needn't show every extreme that they name: `dest`: in the rows of one device (aligned blocks of 64 rows, in order), each owner is named by at most 24 rows, a bound that some block reaches. Let a = k // (256 / (2 * 4)) for a kept id k, and let x-slab p hold x from p * 256 / 4 on, 256 / 4 of them. When a >= 4, the cells on which row a of H(256) is nonzero lie in one x-slab. Among the 64 ids of one y-slab and one index of sta, at most 32 ids with a >= 4 touch any one x-slab, and some x-slab is touched by exactly 32.
All inputs are finite; a program needn't handle non-finite values.
Results may differ from a plain program's by a relative error of at most 0.0003.
Values sent between devices are 32-bit elements; how exact they have to be, the bound alone decides.
A program may use at most 128 MiB of HBM per device.

v0:
```python
import jax
import jax.numpy as jnp
from jax import lax
from jax.sharding import PartitionSpec as P

kernel_scale = 32.0
root_half = 0.7071067811865476


def haar(order):
    matrix = jnp.eye(order, dtype=jnp.float32)
    rows = jnp.arange(order, dtype=jnp.int32)[:, None]
    cols = jnp.arange(order, dtype=jnp.int32)[None, :]
    active = order
    while active % 2 == 0 and active > 1:
        half = active // 2
        low = (rows < half) & ((cols == 2 * rows) | (cols == 2 * rows + 1))
        upper = (rows >= half) & (rows < active)
        plus = upper & (cols == 2 * (rows - half))
        minus = upper & (cols == 2 * (rows - half) + 1)
        keeps = (rows >= active) & (rows == cols)
        step = (
            jnp.where(low | plus, root_half, 0.0)
            - jnp.where(minus, root_half, 0.0)
            + jnp.where(keeps, 1.0, 0.0)
        ).astype(jnp.float32)
        matrix = jnp.dot(
            step, matrix, precision=lax.Precision.HIGHEST, preferred_element_type=jnp.float32
        )
        active = half
    return matrix


def kernel(place, height, weight, xs, nx, ny, nz):
    ys = jnp.arange(ny, dtype=jnp.int32).astype(jnp.float32) + 0.5
    zs = jnp.arange(nz, dtype=jnp.int32).astype(jnp.float32) + 0.5
    east = xs[None, :] - place[:, 0:1] * nx
    north = ys[None, :] - place[:, 1:2] * ny
    depth = zs[None, :] + height[:, None]
    radius = (
        east[:, :, None, None] ** 2 + north[:, None, :, None] ** 2 + depth[:, None, None, :] ** 2
    )
    return kernel_scale * weight[None] * depth[:, None, None, :] / (radius * jnp.sqrt(radius))


def owning_slab(xrows, x_cells, x_local):
    power = jnp.ones_like(xrows)
    width = 2
    while width < x_cells:
        power = jnp.where(xrows >= width, width, power)
        width = width * 2
    return (xrows - power) * (x_cells // power) // x_local


def classify(ids, half, slab_count, x_cells, x_local):
    xrows = ids // half
    fine = xrows >= slab_count
    source = jnp.where(fine, owning_slab(xrows, x_cells, x_local), slab_count)
    labels = jnp.arange(slab_count + 1, dtype=jnp.int32)
    onehot = (source[..., None] == labels).astype(jnp.int32)
    order_in = jnp.sum((jnp.cumsum(onehot, axis=-2) - onehot) * onehot, axis=-1)
    return (fine, source, order_in)


def local(station_place, station_height, cell_weight, kept, dest):
    slab_count = lax.axis_size("slab")
    owner_count = lax.axis_size("sta")
    x_local, y_cells, z_cells = cell_weight.shape
    x_cells = x_local * slab_count
    stations = station_place.shape[0]
    keep = kept.shape[2]
    block = 2 * z_cells
    wx, wy, wz = (haar(x_cells), haar(y_cells), haar(z_cells))
    offset = lax.axis_index("slab") * x_local
    xs = (offset + jnp.arange(x_local, dtype=jnp.int32)).astype(jnp.float32) + 0.5
    field = kernel(station_place, station_height, cell_weight, xs, x_cells, y_cells, z_cells)
    field = jnp.einsum("sxyz,cz->sxyc", field, wz, precision=lax.Precision.HIGHEST)
    field = jnp.einsum("by,sxyc->sxbc", wy, field, precision=lax.Precision.HIGHEST)
    half = y_cells // slab_count // 2
    per_row = stations * keep
    me_slab = lax.axis_index("slab")
    fine_cap = max(2, 2 * per_row // slab_count)
    sums = jnp.sum(field, axis=1) * x_local ** (-0.5)
    arrived_sums = lax.all_to_all(sums[:, None], "slab", split_axis=2, concat_axis=1, tiled=True)
    coarse = jnp.einsum(
        "ap,spyc->sayc", haar(slab_count), arrived_sums, precision=lax.Precision.HIGHEST
    )
    coarse_flat = coarse.reshape(stations, slab_count * half, block)
    all_ids = lax.all_gather(kept, "slab", axis=0, tiled=True).reshape(slab_count, per_row)
    fine, source, order_in = classify(all_ids, half, slab_count, x_cells, x_local)
    is_mine = fine & (source == me_slab)
    slots = jnp.arange(fine_cap, dtype=jnp.int32)
    chosen = is_mine[:, :, None] & (order_in[:, :, None] == slots[None, None, :])
    row_numbers = jnp.arange(per_row, dtype=jnp.int32)[None, :, None]
    row_of = jnp.sum(jnp.where(chosen, row_numbers, 0), axis=1)
    filled = jnp.any(chosen, axis=1)
    ids_taken = jnp.take_along_axis(all_ids, row_of, axis=1)
    station_of = row_of // keep
    slab_ids = jnp.arange(slab_count, dtype=jnp.int32)[:, None]
    ypair = slab_ids * half + ids_taken % half
    paired = field.reshape(stations, x_local, y_cells // 2, block)
    gathered = paired[station_of, :, ypair]
    local_rows = lax.dynamic_slice_in_dim(wx, offset, x_local, 1)
    weights = local_rows[ids_taken // half]
    outgoing = jnp.einsum("jkx,jkxc->jkc", weights, gathered, precision=lax.Precision.HIGHEST)
    outgoing = jnp.where(filled[:, :, None], outgoing, 0.0)
    arrived = lax.all_to_all(outgoing, "slab", split_axis=0, concat_axis=0, tiled=True)
    own_ids = kept[0].reshape(per_row)
    own_fine, own_source, own_order = classify(own_ids, half, slab_count, x_cells, x_local)
    fine_values = arrived[
        jnp.minimum(own_source, slab_count - 1), jnp.minimum(own_order, fine_cap - 1)
    ]
    own_station = jnp.arange(per_row, dtype=jnp.int32) // keep
    coarse_values = coarse_flat[own_station, jnp.where(own_fine, 0, own_ids)]
    picked = jnp.where(own_fine[:, None], fine_values, coarse_values).reshape(stations, keep, block)
    capacity = max(2, 3 * per_row // owner_count)
    owner = dest.reshape(per_row)
    values = picked.reshape(per_row, block)
    owners = jnp.arange(owner_count, dtype=jnp.int32)
    onehot = (owner[:, None] == owners[None, :]).astype(jnp.int32)
    slot = jnp.sum((jnp.cumsum(onehot, axis=0) - onehot) * onehot, axis=1)
    outgoing_rows = (
        jnp.zeros((owner_count, capacity, block), jnp.float32).at[owner, slot].set(values)
    )
    return lax.all_to_all(
        outgoing_rows[None, :, None], "sta", split_axis=1, concat_axis=2, tiled=True
    )


def solution(mesh):
    placed = (
        P("sta", None),
        P("sta"),
        P("slab", None, None),
        P("slab", "sta", None),
        P("slab", "sta", None, None),
    )
    return jax.shard_map(
        local,
        mesh=mesh,
        in_specs=placed,
        out_specs=P("slab", "sta", None, None, None),
        check_vma=False,
    )
```

profile of v0, /device:TPU:0, one launch (start us, length us, event | category | flops | bytes accessed | tf_op | source)
XLA Modules:
  0.0 188.8 jit_solution(8885485338434997958)
XLA Ops:
  0.6 9.7 %all_gather.3 = s32[4,4,16]{2,1,0:T(4,128)S(1)} all-gather(s32[1,4,16]{2,1,0:T(4,128)} %param.8), channel_id=1, replica_groups=mesh['slab'=4,'sta'=8] {'slab'}, dimensions={0}, use_global_device_ids=true | all-gather | bytes 1280 | tf_op jit(solution)/shard_map/all_gather | solution.py:89
  10.4 0.1 compare_and_fusion.6
  10.5 0.1 fusion.164
  10.6 0.1 reduce_window_sum.34
  10.8 0.2 select_reduce_fusion
  11.0 0.2 fusion.190
  11.1 0.2 select_reduce_fusion.1
  11.3 0.8 multiply_bitcast_fusion.2
  12.1 0.1 reshape.1251
  12.2 1.5 gather_fusion.4
  13.9 0.1 reshape.1233
  14.0 0.5 fusion.11
  14.5 0.9 fusion.17
  15.5 0.9 fusion.23
  16.4 0.9 fusion.29
  17.3 0.9 fusion.35
  18.3 0.9 fusion.41
  19.2 0.9 fusion.47
  20.1 0.9 fusion.53
  21.0 0.1 copy.31
  21.1 2.5 %broadcast_multiply_fusion = f32[64,256,64]{1,2,0:T(8,128)S(1)} fusion(f32[64,256,64]{1,2,0:T(8,128)} %param.7), kind=kLoop, calls=%fused_computation.16 | loop fusion | flops 1048576 | bytes 8388608 | tf_op jit(solution)/shard_map/mul | solution.py:43
  23.9 0.1 broadcast_add_fusion
  24.0 0.3 fusion.192
  24.3 0.3 fusion.198
  24.5 0.3 fusion.204
  24.8 0.3 fusion.210
  25.1 0.3 fusion.216
  25.4 0.3 convolution_bitcast_fusion.2
  25.7 24.6 %fusion.1 = f32[4,64,256,64]{2,3,1,0:T(8,128)} fusion(f32[64,64,1,1]{1,0,3,2:T(8,128)S(1)} %convolution_bitcast_fusion.2, f32[4,64]{1,0:T(4,128)S(1)} %get-tuple-element.14, f32[4,64,256]{2,1,0:T(8,128)S(1)} %broadcast_add_fusion, f32[4,64]{1,0:T(4,128)S(1)} %get-tuple-element.13, f32[64,256,64]{1,2,0:T(8,128)S(1)} %broadcast_multiply_fusion), kind=kOutput, calls=%fused_computation.8 | convolution fusion | flops 3238002688 | bytes 21252096 | tf_op jit(solution)/shard_map/sxyz,cz->sxyc/dot_general | solution.py:77
  50.2 18.5 %fusion.479 = (f32[4,256,64]{1,2,0:T(8,128)S(1)}, f32[4,64,256,64]{2,3,1,0:T(8,128)}) fusion(f32[4,64,256,64]{2,3,1,0:T(8,128)} %fusion.1, f32[256,256]{0,1:T(8,128)S(1)} %fusion.53), kind=kOutput, calls=%fused_computation.643 | convolution fusion | flops 12889030656 | bytes 34078720 | tf_op jit(solution)/shard_map/by,sxyc->sxbc/dot_general | solution.py:78
  68.8 22.9 %copy.33 = f32[4,64,256,64]{3,2,1,0:T(8,128)} copy(f32[4,64,256,64]{2,3,1,0:T(8,128)} %get-tuple-element.18) | data formatting | bytes 33554432 | tf_op jit(solution)/shard_map/by,sxyc->sxbc/transpose | solution.py:78
  91.6 26.7 %reshape.1223 = f32[4,64,128,128]{3,2,1,0:T(8,128)} reshape(f32[4,64,256,64]{3,2,1,0:T(8,128)} %copy.33) | data formatting | bytes 33554432 | tf_op jit(solution)/shard_map/reshape | solution.py:101
  118.3 17.7 %copy.34 = f32[4,64,128,128]{3,1,2,0:T(8,128)} copy(f32[4,64,128,128]{3,2,1,0:T(8,128)} %reshape.1223) | data formatting | bytes 33554432 | tf_op jit(solution)/shard_map/reshape | solution.py:101
  136.0 0.6 gather_fusion
  136.7 8.6 %gather_fusion.1 = f32[128,64,128]{2,1,0:T(8,128)} fusion(f32[4,64,128,128]{3,1,2,0:T(8,128)} %copy.34, s32[128]{0:T(128)S(1)} %reshape.1233), kind=kCustom, calls=%fused_computation.1 | custom fusion | bytes 8389632 | tf_op jit(solution)/shard_map/gather | solution.py:102
  145.3 5.3 %fusion.480 = f32[4,32,1,128]{3,2,1,0:T(1,128)S(1)} fusion(f32[4,32,64,1]{2,3,1,0:T(1,128)S(1)} %bitcast.113, f32[4,32,64,128]{3,2,1,0:T(8,128)} %bitcast.108), kind=kOutput, calls=%fused_computation.644 | convolution fusion | flops 12582912 | bytes 4292608 | tf_op jit(solution)/shard_map/jkx,jkxc->jkc/dot_general | solution.py:105
  150.5 0.7 broadcast_select_fusion
  151.3 3.3 %all-to-all-start = ((f32[4,32,128]{2,1,0:T(8,128)}), f32[4,32,128]{2,1,0:T(8,128)S(1)}, u32[]{:S(2)}, u32[]{:S(2)}) async-start(f32[4,32,128]{2,1,0:T(8,128)} %broadcast_select_fusion), calls=%async_computation | async-start | bytes 131072 | tf_op jit(solution)/shard_map/all_to_all | solution.py:107
  154.9 0.1 fusion.400
  155.1 0.1 reduce_window_sum.35
  155.2 0.2 select_reduce_fusion.2
  155.5 0.1 reduce_window_sum.33
  155.6 0.1 fusion.401
  155.8 0.2 fusion.337
  156.0 0.2 convolution_bitcast_fusion.3
  156.2 0.2 select_reduce_fusion.3
  156.4 0.6 broadcast.2377
  156.9 0.6 reduce.5
  157.6 0.1 reshape.1221
  157.7 0.2 copy.35
  157.9 1.2 reshape.1282
  159.1 0.3 all-to-all-done
  159.4 3.9 %all-to-all-start.1 = ((f32[4,1,16384]{2,1,0:T(1,128)}), f32[4,1,16384]{2,1,0:T(1,128)S(1)}, u32[]{:S(2)}, u32[]{:S(2)}) async-start(f32[4,1,16384]{2,1,0:T(1,128)} %reshape.1282), calls=%async_computation.1 | async-start | bytes 524288 | tf_op jit(solution)/shard_map/all_to_all | solution.py:84
  163.3 0.9 gather_fusion.2
  164.1 4.5 %all-to-all-done.1 = f32[4,1,16384]{2,1,0:T(1,128)S(1)} async-done(((f32[4,1,16384]{2,1,0:T(1,128)}), f32[4,1,16384]{2,1,0:T(1,128)S(1)}, u32[]{:S(2)}, u32[]{:S(2)}) %all-to-all-start.1) | async-done | bytes 262176 | tf_op jit(solution)/shard_map/all_to_all | solution.py:84
  168.6 0.5 broadcast.2385
  169.1 1.4 reduce.6
  170.5 0.4 reshape.1283
  170.9 1.3 convolution_bitcast_fusion.1
  172.3 0.1 reshape.1224
  172.4 0.9 gather_fusion.3
  173.4 3.8 %scatter_fusion = f32[8,24,128]{2,1,0:T(8,128)S(1)} fusion(f32[8,24,128]{2,1,0:T(8,128)S(1)} %broadcast_in_dim.272, s32[64]{0:T(128)S(1)} %fusion.402, f32[64,128]{1,0:T(8,128)S(1)} %broadcast_select_fusion.1), kind=kCustom, calls=%fused_computation.5 | custom fusion | bytes 98816 | tf_op jit(solution)/shard_map/scatter | solution.py:123
  177.2 11.0 %all_to_all.29 = f32[1,8,1,24,128]{4,3,2,0,1:T(8,128)S(1)} all-to-all(f32[1,8,1,24,128]{4,3,2,0,1:T(8,128)S(1)} %bitcast.109), channel_id=1, replica_groups=mesh['slab'=4,'sta'=8] {'sta'}, dimensions={1} | all-to-all | bytes 196608 | tf_op jit(solution)/shard_map/all_to_all | solution.py:125
  188.1 0.6 copy.51
  (83 shorter events, 1.5 us)
Async XLA Ops:
  0.0 23.8 %copy-start.2 = (f32[4]{0:T(128)S(1)}, f32[4]{0:T(128)}, u32[]{:S(2)}) copy-start(f32[4]{0:T(128)} %param.6) | copy-start | bytes 52
  118.3 36.2 %copy-start = (s32[1,4,16]{2,1,0:T(4,128)S(1)}, s32[1,4,16]{2,1,0:T(4,128)}, u32[]{:S(2)}) copy-start(s32[1,4,16]{2,1,0:T(4,128)} %param.8) | copy-start | bytes 772
  118.3 36.5 %copy-start.1 = (s32[1,4,16,1]{2,3,1,0:T(1,128)S(1)}, s32[1,4,16,1]{2,3,1,0:T(1,128)}, u32[]{:S(2)}) copy-start(s32[1,4,16,1]{2,3,1,0:T(1,128)} %param.9) | copy-start | bytes 772
  151.3 8.1 %all-to-all-start = ((f32[4,32,128]{2,1,0:T(8,128)}), f32[4,32,128]{2,1,0:T(8,128)S(1)}, u32[]{:S(2)}, u32[]{:S(2)}) async-start(f32[4,32,128]{2,1,0:T(8,128)} %broadcast_select_fusion), calls=%async_computation | async-start | bytes 131072 | tf_op jit(solution)/shard_map/all_to_all | solution.py:107
  159.4 9.3 %all-to-all-start.1 = ((f32[4,1,16384]{2,1,0:T(1,128)}), f32[4,1,16384]{2,1,0:T(1,128)S(1)}, u32[]{:S(2)}, u32[]{:S(2)}) async-start(f32[4,1,16384]{2,1,0:T(1,128)} %reshape.1282), calls=%async_computation.1 | async-start | bytes 524288 | tf_op jit(solution)/shard_map/all_to_all | solution.py:84
where the time goes:
time: 191 us; the launch traced here: 189 us
  local copies, waits for them, and re-layouts  88.1 us (46%)
  matrix products  58.6 us (31%)
  blocking collectives  20.7 us (11%)
  other arithmetic  8.82 us (5%)
  starting transfers between devices  7.17 us (4%)
  waiting for transfers between devices  4.75 us (2%)
    reshape x2, local copies, waits for them, and re-layouts, local(): paired = field.reshape(stations, x_local, y_cells // 2, block)  44.4 us
    dot_general x1, matrix products, local(): jnp.einsum('sxyz,cz->sxyc', field, wz, precision=lax.Precision.HIGHEST)  24.6 us
    transpose x1, local copies, waits for them, and re-layouts, local(): jnp.einsum('by,sxyc->sxbc', wy, field, precision=lax.Precision.HIGHEST)  22.9 us
    dot_general x1, matrix products, local(): jnp.einsum('by,sxyc->sxbc', wy, field, precision=lax.Precision.HIGHEST)  18.5 us
    all_to_all x1, blocking collectives, local(): lax.all_to_all(outgoing_rows[None, :, None], 'sta', split_axis=1, concat_...  11 us
    all_gather x1, blocking collectives, local(): lax.all_gather(kept, 'slab', axis=0, tiled=True)  9.71 us
    dot_general x16, matrix products, haar(): jnp.dot(step, matrix, precision=lax.Precision.HIGHEST, preferred_element_...  8.93 us
    gather x1, local copies, waits for them, and re-layouts, local(): gathered = paired[station_of, :, ypair]  8.58 us
  transfers between devices with their start and end apart: 2, of which 2 were waited for; matrix products, arithmetic and copies ran while one was open for 3% of the time, Pallas kernels for 0%

commit v1 on v0

v1 whole, which is shorter than its diff:
```python
import functools
import math

import jax
import jax.numpy as jnp
from jax import lax
from jax.experimental import pallas as pl
from jax.experimental.pallas import tpu as pltpu
from jax.sharding import PartitionSpec as P

kernel_scale = 32.0
MESH = pl.DeviceIdType.MESH


def log2(n):
    return n.bit_length() - 1


def row_plan(ids, j, me, slab, half, x_cells, y_cells):
    ls = log2(slab)
    a = ids >> log2(half)
    pair = j * half + (ids & (half - 1))
    here = jnp.zeros_like(a)
    factor = jnp.full(a.shape, x_cells ** -0.5, jnp.float32)
    m = 1
    while m < x_cells:
        e = log2(m)
        at = a >= m
        k = a - m
        norm = (m / x_cells) ** 0.5
        if m >= slab:
            sh = e - ls
            mine = (k >> sh) == me
            here = jnp.where(at, (m >> ls) + (k & ((1 << sh) - 1)), here)
            factor = jnp.where(at, jnp.where(mine, norm, 0.0), factor)
        else:
            sh = ls - e
            mine = k == (me >> sh)
            sign = norm * (1 - 2 * ((me >> (sh - 1)) & 1)).astype(jnp.float32)
            factor = jnp.where(at, jnp.where(mine, sign, 0.0), factor)
        m = m * 2
    ynorm = jnp.full(a.shape, y_cells ** -0.5, jnp.float32)
    m = 1
    while m < y_cells // 2:
        ynorm = jnp.where(pair >= m, (2 * m / y_cells) ** 0.5, ynorm)
        m = m * 2
    return here * y_cells + 2 * pair, factor * ynorm


def z_matrix(z_cells, t):
    z = lax.broadcasted_iota(jnp.int32, (2 * z_cells, 2 * z_cells), 0) & (z_cells - 1)
    lane = lax.broadcasted_iota(jnp.int32, (2 * z_cells, 2 * z_cells), 1)
    c = lane & (z_cells - 1)
    value = jnp.full(z.shape, z_cells ** -0.5, jnp.float32)
    m = 1
    while m < z_cells:
        w = log2(z_cells // m)
        k = c - m
        norm = (m / z_cells) ** 0.5
        hit = (z >> w) == k
        up = ((z >> (w - 1)) & 1) == 0
        value = jnp.where(c >= m, jnp.where(hit, jnp.where(up, norm, -norm), 0.0), value)
        m = m * 2
    return jnp.where((lane >> log2(z_cells)) == t, value, 0.0)


def tree(values):
    out = [None] * len(values)
    while len(values) > 1:
        half = len(values) // 2
        for k in range(half):
            out[half + k] = values[2 * k] - values[2 * k + 1]
        values = [values[2 * k] + values[2 * k + 1] for k in range(half)]
    out[0] = values[0]
    return out


GROUP = 4


def local_kernel(sizes, place, height, w_ref, ids_ref, out_ref, field, twice, table, rows_v, rows_s, taken, sem):
    slab, stations, keep, x_local, y_cells, z_cells, chunk = sizes
    lanes = 2 * z_cells
    pairs = stations // 2
    x_cells = x_local * slab
    half = y_cells // slab // 2
    per_row = stations * keep
    runs = y_cells // 8
    step = pl.program_id(0)
    me = lax.axis_index("slab")
    plane = x_local * y_cells
    left = lax.broadcasted_iota(jnp.int32, (8, lanes), 1) < z_cells
    zed = (lax.broadcasted_iota(jnp.int32, (8, lanes), 1) & (z_cells - 1)).astype(jnp.float32) + 0.5

    def two(pair, of):
        return jnp.where(left, of(2 * pair), of(2 * pair + 1))

    depths = [zed + two(p, lambda s: height[s]) for p in range(pairs)]

    @pl.when(step == 0)
    def _():
        for j in range(slab):
            where_from, _ = row_plan(ids_ref[j : j + 1, :], j, me, slab, half, x_cells, y_cells)
            rows_v[j : j + 1, :] = where_from
        copy = pltpu.make_async_copy(rows_v, rows_s, sem)
        copy.start()
        base = (lax.broadcasted_iota(jnp.int32, (8, lanes), 0) * runs).astype(jnp.float32) + 0.5
        for p in range(pairs):
            square = depths[p] * depths[p]
            north = base - two(p, lambda s: place[s, 1] * y_cells)
            for r in range(runs):
                n = north + float(r)
                table[p, r] = n * n + square
        copy.wait()

    first = step * chunk
    for u in range(chunk):
        wide = w_ref[u]
        twice[pl.ds(u * y_cells, y_cells), :] = jnp.concatenate([wide, wide], axis=1)

    def group(g, carry):
        x0 = first + g * GROUP
        for p in range(pairs):
            easts = []
            for u in range(GROUP):
                x = (me * x_local + x0 + u).astype(jnp.float32) + 0.5
                e = x - two(p, lambda s: place[s, 0] * x_cells)
                easts.append(e * e)

            def emit(level, run, values):
                if level is None:
                    start, stride = 0, 1
                else:
                    stride = runs >> level
                    start = (y_cells >> level) + run
                out = tree(values)
                for h in range(GROUP):
                    if h == 0:
                        xrow = x0 // GROUP
                    else:
                        m = 1 << log2(h)
                        xrow = x_local * m // GROUP + (x0 * m // GROUP) + (h - m)
                    at = p * plane + xrow * y_cells + start
                    if stride == 1:
                        field[pl.ds(at, 8), :] = out[h]
                    else:
                        field[pl.ds(at, 8, stride=stride), :] = out[h]

            stack = []
            for r in range(runs):
                t = table[p, r]
                values = []
                for u in range(GROUP):
                    inv = lax.rsqrt(t + easts[u])
                    w = twice[pl.ds((g * GROUP + u) * y_cells + r, 8, stride=runs), :]
                    values.append((w * inv) * (inv * inv))
                level, run = 0, r
                while stack and stack[-1][0] == level:
                    _, other = stack.pop()
                    level, run = level + 1, run >> 1
                    emit(level, run, [o - v for o, v in zip(other, values)])
                    values = [o + v for o, v in zip(other, values)]
                stack.append((level, values))
            emit(None, 0, stack[0][1])
        return carry

    lax.fori_loop(0, chunk // GROUP, group, 0)

    @pl.when(step == pl.num_programs(0) - 1)
    def _():
        coarse = x_local // GROUP

        def finish_x(tile, carry):
            for p in range(pairs):
                at = [p * plane + x * y_cells + tile * 8 for x in range(coarse)]
                values = tree([field[pl.ds(pl.multiple_of(a, 8), 8), :] for a in at])
                for a, v in zip(at, values):
                    field[pl.ds(pl.multiple_of(a, 8), 8), :] = v
            return carry

        lax.fori_loop(0, runs, finish_x, 0)

        def finish_y(block, carry):
            for p in range(pairs):
                at = p * plane + block * (8 * y_cells)
                values = tree([field[pl.ds(at + i, 8, stride=y_cells), :] for i in range(8)])
                for i in range(8):
                    field[pl.ds(at + i, 8, stride=y_cells), :] = values[i]
            return carry

        lax.fori_loop(0, x_local // 8, finish_y, 0)
        even, odd = z_matrix(z_cells, 0), z_matrix(z_cells, 1)
        eye = lax.broadcasted_iota(jnp.int32, (per_row, per_row), 0) == lax.broadcasted_iota(
            jnp.int32, (per_row, per_row), 1
        )
        side = lax.broadcasted_iota(jnp.int32, (1, lanes), 1) < z_cells

        def one_slab(j, carry):
            for s in range(stations):
                for i in range(keep):
                    k = s * keep + i
                    at = (s // 2) * plane + rows_s[j, k]
                    taken[2 * k : 2 * k + 2, :] = field[pl.ds(at, 2), :]
            scales = []
            for s in range(stations):
                d = kernel_scale * depths[s // 2][0:1, :]
                d = jnp.where(side if s % 2 == 0 else jnp.logical_not(side), d, 0.0)
                scales.append(jnp.broadcast_to(d, (keep, lanes)))
            scale = jnp.concatenate(scales, axis=0)
            _, factor = row_plan(ids_ref[pl.ds(j, 1), :], j, me, slab, half, x_cells, y_cells)
            factor = jnp.sum(jnp.where(eye, factor, 0.0), axis=1, keepdims=True)
            scale = scale * factor
            x_even = taken[pl.ds(0, per_row, stride=2), :] * scale
            x_odd = taken[pl.ds(1, per_row, stride=2), :] * scale
            out_ref[j] = jnp.dot(
                x_even, even, precision=lax.Precision.HIGHEST, preferred_element_type=jnp.float32
            ) + jnp.dot(x_odd, odd, precision=lax.Precision.HIGHEST, preferred_element_type=jnp.float32)
            return carry

        lax.fori_loop(0, slab, one_slab, 0)


def send_kernel(sizes, parts, dest, out, arrived, packed, s_send, s_recv, o_send, o_recv, own_sem):
    slab, owners, per_row, capacity = sizes
    me, q = lax.axis_index("slab"), lax.axis_index("sta")
    barrier = pltpu.get_barrier_semaphore()
    for d in range(1, slab):
        to = lax.rem(me + d, slab)
        pl.semaphore_signal(barrier, inc=1, device_id=(to, q), device_id_type=MESH)
    for d in range(1, owners):
        to = lax.rem(q + d, owners)
        pl.semaphore_signal(barrier, inc=1, device_id=(me, to), device_id_type=MESH)
    pl.semaphore_wait(barrier, slab + owners - 2)
    copies = []
    for d in range(1, slab):
        to = lax.rem(me + d, slab)
        copy = pltpu.make_async_remote_copy(
            src_ref=parts.at[to],
            dst_ref=arrived.at[d - 1],
            send_sem=s_send.at[d - 1],
            recv_sem=s_recv.at[d - 1],
            device_id=(to, q),
            device_id_type=MESH,
        )
        copy.start()
        copies.append(copy)
    owner = dest[...]
    names = lax.broadcasted_iota(jnp.int32, (owners, per_row), 0)
    named = (names == owner).astype(jnp.float32)
    before = (
        lax.broadcasted_iota(jnp.int32, (per_row, per_row), 0)
        < lax.broadcasted_iota(jnp.int32, (per_row, per_row), 1)
    ).astype(jnp.float32)
    rank = jnp.dot(named, before, preferred_element_type=jnp.float32)
    slot = jnp.sum(rank * named, axis=0, keepdims=True)
    spot = owner.astype(jnp.float32) * capacity + slot
    rows = lax.broadcasted_iota(jnp.int32, (owners * capacity, per_row), 0).astype(jnp.float32)
    select = (rows == spot).astype(jnp.float32)
    total = parts[me]
    for copy in copies:
        copy.wait()
    for d in range(1, slab):
        total = total + arrived[d - 1]
    packed[...] = jnp.dot(
        select, total, precision=lax.Precision.HIGHEST, preferred_element_type=jnp.float32
    ).reshape(packed.shape)
    copies = []
    for d in range(1, owners):
        to = lax.rem(q + d, owners)
        copy = pltpu.make_async_remote_copy(
            src_ref=packed.at[to],
            dst_ref=out.at[q],
            send_sem=o_send.at[d - 1],
            recv_sem=o_recv.at[d - 1],
            device_id=(me, to),
            device_id_type=MESH,
        )
        copy.start()
        copies.append(copy)
    own = pltpu.make_async_copy(packed.at[q], out.at[q], own_sem)
    own.start()
    own.wait()
    for copy in copies:
        copy.wait()


def local(station_place, station_height, cell_weight, kept, dest):
    slab = lax.axis_size("slab")
    owners = lax.axis_size("sta")
    x_local, y_cells, z_cells = cell_weight.shape
    stations = station_place.shape[0]
    keep = kept.shape[2]
    lanes = 2 * z_cells
    per_row = stations * keep
    capacity = max(2, 3 * per_row // owners)
    chunk = 8
    ids = lax.all_gather(kept, "slab", axis=0, tiled=True).reshape(slab, per_row)
    sizes = (slab, stations, keep, x_local, y_cells, z_cells, chunk)
    pairs = stations // 2
    parts = pl.pallas_call(
        functools.partial(local_kernel, sizes),
        grid=(x_local // chunk,),
        out_shape=jax.ShapeDtypeStruct((slab, per_row, lanes), jnp.float32),
        in_specs=[
            pl.BlockSpec(memory_space=pltpu.SMEM),
            pl.BlockSpec(memory_space=pltpu.SMEM),
            pl.BlockSpec((chunk, y_cells, z_cells), lambda i: (i, 0, 0)),
            pl.BlockSpec((slab, per_row), lambda i: (0, 0)),
        ],
        out_specs=pl.BlockSpec((slab, per_row, lanes), lambda i: (0, 0, 0)),
        scratch_shapes=[
            pltpu.VMEM((pairs * x_local * y_cells, lanes), jnp.float32),
            pltpu.VMEM((chunk * y_cells, lanes), jnp.float32),
            pltpu.VMEM((pairs, y_cells // 8, 8, lanes), jnp.float32),
            pltpu.VMEM((slab, per_row), jnp.int32),
            pltpu.SMEM((slab, per_row), jnp.int32),
            pltpu.VMEM((2 * per_row, lanes), jnp.float32),
            pltpu.SemaphoreType.DMA,
        ],
        compiler_params=pltpu.CompilerParams(vmem_limit_bytes=48 * 2**20),
    )(station_place, station_height, cell_weight, ids)
    out = pl.pallas_call(
        functools.partial(send_kernel, (slab, owners, per_row, capacity)),
        out_shape=jax.ShapeDtypeStruct((owners, capacity, lanes), jnp.float32),
        in_specs=[pl.BlockSpec(memory_space=pltpu.VMEM)] * 2,
        out_specs=pl.BlockSpec(memory_space=pltpu.VMEM),
        scratch_shapes=[
            pltpu.VMEM((slab - 1, per_row, lanes), jnp.float32),
            pltpu.VMEM((owners, capacity, lanes), jnp.float32),
            pltpu.SemaphoreType.DMA((slab - 1,)),
            pltpu.SemaphoreType.DMA((slab - 1,)),
            pltpu.SemaphoreType.DMA((owners - 1,)),
            pltpu.SemaphoreType.DMA((owners - 1,)),
            pltpu.SemaphoreType.DMA,
        ],
        compiler_params=pltpu.CompilerParams(collective_id=0, has_side_effects=True),
    )(parts, dest.reshape(1, per_row))
    return out.reshape(1, 1, owners, capacity, lanes)


def solution(mesh):
    placed = (
        P("sta", None),
        P("sta"),
        P("slab", None, None),
        P("slab", "sta", None),
        P("slab", "sta", None, None),
    )
    return jax.shard_map(
        local,
        mesh=mesh,
        in_specs=placed,
        out_specs=P("slab", "sta", None, None, None),
        check_vma=False,
    )
```

time: 191 us -> 56.1 us (0.29); the launches traced: 189 us -> 55.8 us
  local copies, waits for them, and re-layouts: 88.1 us -> 10.4 us
  matrix products: 58.6 us -> 0 us
  Pallas kernels: 0 us -> 35.1 us
  blocking collectives: 20.7 us -> 9.56 us
  other arithmetic: 8.82 us -> 0.66 us
  starting transfers between devices: 7.17 us -> 0 us
  waiting for transfers between devices: 4.75 us -> 0 us
    dot_general x20 -> x0, matrix products: 58.6 us -> none  [the longest x1 24.6 us: local(): jnp.einsum('sxyz,cz->sxyc', field, wz, precision=lax.Precision.HIGHEST)]
    reshape x5 -> x2, local copies, waits for them, and re-layouts: 44.7 us -> 0.68 us  [the longest x1 0.6 us: local(): dest.reshape(1, per_row)]
    pallas_call x0 -> x2, Pallas kernels: none -> 35.1 us  [the longest x1 22.7 us: local(): pl.pallas_call(functools.partial(local_kernel, sizes), grid=(x_local // c...]
    transpose x2 -> x0, local copies, waits for them, and re-layouts: 22.9 us -> none  [the longest x1 22.9 us: local(): jnp.einsum('by,sxyc->sxbc', wy, field, precision=lax.Precision.HIGHEST)]
    gather x7 -> x0, local copies, waits for them, and re-layouts: 12.7 us -> none  [the longest x1 8.58 us: local(): gathered = paired[station_of, :, ypair]]
    all_to_all x1 -> x0, blocking collectives: 11 us -> none  [local(): lax.all_to_all(outgoing_rows[None, :, None], 'sta', split_axis=1, concat_...]
    all_to_all x2 -> x0, starting transfers between devices: 7.17 us -> none  [the longest x1 3.88 us: local(): lax.all_to_all(sums[:, None], 'slab', split_axis=2, concat_axis=1, tiled=...]
    unnamed x10 -> x14, local copies, waits for them, and re-layouts: 2.78 us -> 9.75 us
  transfers between devices with their start and end apart: 2 -> 0, of which waited for: 2 -> 0; matrix products, arithmetic and copies ran while one was open for 3% -> 0% of each run, Pallas kernels for 0% -> 0%
where the time goes in v1:
time: 56.1 us; the launch traced here: 55.8 us
  Pallas kernels  35.1 us (63%)
  local copies, waits for them, and re-layouts  10.4 us (19%)
  blocking collectives  9.56 us (17%)
  other arithmetic  0.66 us (1%)
    pallas_call x1, Pallas kernels, local(): pl.pallas_call(functools.partial(local_kernel, sizes), grid=(x_local // c...  22.7 us
    pallas_call x1, Pallas kernels, local(): pl.pallas_call(functools.partial(send_kernel, (slab, owners, per_row, cap...  12.5 us
    unnamed x14, local copies, waits for them, and re-layouts  9.75 us
    all_gather x1, blocking collectives, local(): lax.all_gather(kept, 'slab', axis=0, tiled=True).reshape(slab, per_row)  9.56 us

profile of v1, /device:TPU:0, one launch (start us, length us, event | category | flops | bytes accessed | tf_op | source)
XLA Modules:
  0.0 55.8 jit_solution(13591401122098049585)
XLA Ops:
  0.0 0.0 copy-start.2
  0.0 0.0 copy-start.4
  0.0 0.0 copy-start.1
  0.0 0.0 copy-start.3
  0.0 7.0 %copy.9.w_ref = f32[64,256,64]{2,1,0:T(8,128)} copy(f32[64,256,64]{1,2,0:T(8,128)} %param.7) | data formatting | bytes 8388608 | tf_op args[2]
  7.0 0.0 copy-done.2
  7.0 9.6 %all_gather.3 = s32[4,4,16]{2,1,0:T(4,128)S(1)} all-gather(s32[1,4,16]{2,1,0:T(4,128)S(1)} %copy-done.2), channel_id=1, replica_groups=mesh['slab'=4,'sta'=8] {'slab'}, dimensions={0}, use_global_device_ids=true | all-gather | bytes 1280 | tf_op jit(solution)/shard_map/all_gather | solution.py:297
  16.5 0.1 reshape.9.ids_ref
  16.6 0.0 copy-done.4
  16.6 0.1 copy.8.place
  16.7 0.0 copy-done.1
  16.7 22.7 %shard_map.55.parts = f32[4,64,128]{2,1,0:T(8,128)S(1)} custom-call(f32[4,2]{1,0:T(4,128)S(1)} %copy.8.place, f32[4]{0:T(128)S(1)} %copy-done.1, f32[64,256,64]{2,1,0:T(8,128)} %copy.9.w_ref, s32[4,64]{1,0:T(4,128)S(1)} %reshape.9.ids_ref), custom_call_target="tpu_custom_call" | custom-call | tf_op jit(solution)/shard_map/pallas_call | solution.py:300
  39.4 0.0 copy-start
  39.4 0.6 %copy-done = f32[4,64,128]{2,1,0:T(8,128)} copy-done((f32[4,64,128]{2,1,0:T(8,128)}, f32[4,64,128]{2,1,0:T(8,128)S(1)}, u32[]{:S(2)}) %copy-start) | copy-done | bytes 131096
  40.0 0.5 broadcast.3
  40.6 0.0 copy-done.3
  40.6 0.7 %reduce.3 = s32[4,16]{1,0:T(4,128)S(1)} reduce(s32[1,4,16,1]{2,3,1,0:T(1,128)S(1)} %copy-done.3, s32[]{:T(128)} %broadcast.3), dimensions={0,3}, to_apply=%param.9.reduce_sub_computation.3 | reduce | bytes 516 | tf_op args[4]
  41.2 0.6 %reshape.10.dest = s32[1,64]{1,0:T(1,128)} reshape(s32[4,16]{1,0:T(4,128)S(1)} %reduce.3) | data formatting | bytes 512 | tf_op jit(solution)/shard_map/reshape | solution.py:337
  41.8 12.5 %shard_map.56 = f32[8,24,128]{2,1,0:T(8,128)} custom-call(f32[4,64,128]{2,1,0:T(8,128)} %copy-done, s32[1,64]{1,0:T(1,128)} %reshape.10.dest), custom_call_target="tpu_custom_call" | custom-call | tf_op jit(solution)/shard_map/pallas_call | solution.py:322
  54.3 1.5 %copy.11 = f32[1,1,8,24,128]{4,3,2,1,0:T(8,128)} copy(f32[1,1,8,24,128]{4,3,2,1,0:T(8,128)} %bitcast.2) | data formatting | bytes 196608
Async XLA Ops:
  0.0 7.0 %copy-start.2 = (s32[1,4,16]{2,1,0:T(4,128)S(1)}, s32[1,4,16]{2,1,0:T(4,128)}, u32[]{:S(2)}) copy-start(s32[1,4,16]{2,1,0:T(4,128)} %param.8) | copy-start | bytes 772
  0.0 16.6 %copy-start.4 = (f32[4,2]{0,1:T(2,128)S(1)}, f32[4,2]{0,1:T(2,128)}, u32[]{:S(2)}) copy-start(f32[4,2]{0,1:T(2,128)} %param.5) | copy-start | bytes 100
  0.0 16.7 %copy-start.1 = (f32[4]{0:T(128)S(1)}, f32[4]{0:T(128)}, u32[]{:S(2)}) copy-start(f32[4]{0:T(128)} %height.1) | copy-start | bytes 52
  0.0 40.5 %copy-start.3 = (s32[1,4,16,1]{2,3,1,0:T(1,128)S(1)}, s32[1,4,16,1]{2,3,1,0:T(1,128)}, u32[]{:S(2)}) copy-start(s32[1,4,16,1]{2,3,1,0:T(1,128)} %param.9) | copy-start | bytes 772
  39.4 0.6 %copy-start = (f32[4,64,128]{2,1,0:T(8,128)}, f32[4,64,128]{2,1,0:T(8,128)S(1)}, u32[]{:S(2)}) copy-start(f32[4,64,128]{2,1,0:T(8,128)S(1)} %shard_map.55.parts) | copy-start | bytes 393220

commit v2 on v1

v2 whole, which is shorter than its diff:
```python
import functools

import jax
import jax.numpy as jnp
from jax import lax
from jax.experimental import pallas as pl
from jax.experimental.pallas import tpu as pltpu
from jax.sharding import PartitionSpec as P

kernel_scale = 32.0
MESH = pl.DeviceIdType.MESH


def log2(n):
    return n.bit_length() - 1


def row_plan(ids, j, me, slab, half, x_cells, y_cells):
    ls = log2(slab)
    a = ids >> log2(half)
    pair = j * half + (ids & (half - 1))
    here = jnp.zeros_like(a)
    factor = jnp.full(a.shape, x_cells ** -0.5, jnp.float32)
    m = 1
    while m < x_cells:
        e = log2(m)
        at = a >= m
        k = a - m
        norm = (m / x_cells) ** 0.5
        if m >= slab:
            sh = e - ls
            mine = (k >> sh) == me
            here = jnp.where(at, (m >> ls) + (k & ((1 << sh) - 1)), here)
            factor = jnp.where(at, jnp.where(mine, norm, 0.0), factor)
        else:
            sh = ls - e
            mine = k == (me >> sh)
            sign = norm * (1 - 2 * ((me >> (sh - 1)) & 1)).astype(jnp.float32)
            factor = jnp.where(at, jnp.where(mine, sign, 0.0), factor)
        m = m * 2
    ynorm = jnp.full(a.shape, y_cells ** -0.5, jnp.float32)
    m = 1
    while m < y_cells // 2:
        ynorm = jnp.where(pair >= m, (2 * m / y_cells) ** 0.5, ynorm)
        m = m * 2
    return here * y_cells + 2 * pair, factor * ynorm


def z_matrix(z_cells, t):
    z = lax.broadcasted_iota(jnp.int32, (2 * z_cells, 2 * z_cells), 0) & (z_cells - 1)
    lane = lax.broadcasted_iota(jnp.int32, (2 * z_cells, 2 * z_cells), 1)
    c = lane & (z_cells - 1)
    value = jnp.full(z.shape, z_cells ** -0.5, jnp.float32)
    m = 1
    while m < z_cells:
        w = log2(z_cells // m)
        k = c - m
        norm = (m / z_cells) ** 0.5
        hit = (z >> w) == k
        up = ((z >> (w - 1)) & 1) == 0
        value = jnp.where(c >= m, jnp.where(hit, jnp.where(up, norm, -norm), 0.0), value)
        m = m * 2
    return jnp.where((lane >> log2(z_cells)) == t, value, 0.0)


def tree(values):
    out = [None] * len(values)
    while len(values) > 1:
        half = len(values) // 2
        for k in range(half):
            out[half + k] = values[2 * k] - values[2 * k + 1]
        values = [values[2 * k] + values[2 * k + 1] for k in range(half)]
    out[0] = values[0]
    return out


GROUP = 4


def whole_kernel(
    sizes, place, height, w_ref, kept, dest, out,
    field, twice, table, select, others, rows_v, rows_s, taken, parts, arrived, packed,
    row_sem, i_send, i_recv, s_send, s_recv, o_send, o_recv, own_sem,
):
    slab, owners, stations, keep, x_local, y_cells, z_cells, chunk, capacity = sizes
    lanes = 2 * z_cells
    pairs = stations // 2
    x_cells = x_local * slab
    half = y_cells // slab // 2
    per_row = stations * keep
    runs = y_cells // 8
    step = pl.program_id(0)
    last = pl.num_programs(0) - 1
    me, q = lax.axis_index("slab"), lax.axis_index("sta")
    plane = x_local * y_cells
    left = lax.broadcasted_iota(jnp.int32, (8, lanes), 1) < z_cells
    zed = (lax.broadcasted_iota(jnp.int32, (8, lanes), 1) & (z_cells - 1)).astype(jnp.float32) + 0.5

    def two(pair, of):
        return jnp.where(left, of(2 * pair), of(2 * pair + 1))

    depths = [zed + two(p, lambda s: height[s]) for p in range(pairs)]

    def before(d):
        return lax.rem(me - d + slab, slab)

    def id_copy(d):
        return pltpu.make_async_remote_copy(
            src_ref=kept.at[0],
            dst_ref=others.at[d - 1],
            send_sem=i_send.at[d - 1],
            recv_sem=i_recv.at[d - 1],
            device_id=(lax.rem(me + d, slab), q),
            device_id_type=MESH,
        )

    def part_copy(d):
        return pltpu.make_async_remote_copy(
            src_ref=parts.at[d],
            dst_ref=arrived.at[d - 1],
            send_sem=s_send.at[d - 1],
            recv_sem=s_recv.at[d - 1],
            device_id=(before(d), q),
            device_id_type=MESH,
        )

    def out_copy(d):
        to = lax.rem(q + d, owners)
        return pltpu.make_async_remote_copy(
            src_ref=packed.at[to],
            dst_ref=out.at[q],
            send_sem=o_send.at[d - 1],
            recv_sem=o_recv.at[d - 1],
            device_id=(me, to),
            device_id_type=MESH,
        )

    def row_copy():
        return pltpu.make_async_copy(rows_v, rows_s, row_sem)

    @pl.when(step == 0)
    def _():
        barrier = pltpu.get_barrier_semaphore()
        for d in range(1, slab):
            pl.semaphore_signal(
                barrier, inc=1, device_id=(lax.rem(me + d, slab), q), device_id_type=MESH
            )
        for d in range(1, owners):
            pl.semaphore_signal(
                barrier, inc=1, device_id=(me, lax.rem(q + d, owners)), device_id_type=MESH
            )
        base = (lax.broadcasted_iota(jnp.int32, (8, lanes), 0) * runs).astype(jnp.float32) + 0.5
        for p in range(pairs):
            square = depths[p] * depths[p]
            north = base - two(p, lambda s: place[s, 1] * y_cells)
            for r in range(runs):
                n = north + float(r)
                table[p, r] = n * n + square
        owner = jnp.zeros((1, per_row), jnp.float32)
        for s in range(stations):
            spread = lax.broadcasted_iota(jnp.int32, (keep, per_row), 1) == (
                lax.broadcasted_iota(jnp.int32, (keep, per_row), 0) + s * keep
            )
            owner = owner + jnp.dot(
                dest[s].astype(jnp.float32), spread.astype(jnp.float32),
                preferred_element_type=jnp.float32,
            )
        names = lax.broadcasted_iota(jnp.int32, (owners, per_row), 0).astype(jnp.float32)
        named = (names == owner).astype(jnp.float32)
        earlier = (
            lax.broadcasted_iota(jnp.int32, (per_row, per_row), 0)
            < lax.broadcasted_iota(jnp.int32, (per_row, per_row), 1)
        ).astype(jnp.float32)
        rank = jnp.dot(named, earlier, preferred_element_type=jnp.float32)
        slot = jnp.sum(rank * named, axis=0, keepdims=True)
        spot = owner * capacity + slot
        rows = lax.broadcasted_iota(jnp.int32, (owners * capacity, per_row), 0).astype(jnp.float32)
        select[...] = (rows == spot).astype(jnp.float32)
        pl.semaphore_wait(barrier, slab + owners - 2)
        for d in range(1, slab):
            id_copy(d).start()

    @pl.when(step == last)
    def _():
        for d in range(1, slab):
            id_copy(d).wait()
        for d in range(slab):
            ids = kept[0] if d == 0 else others[d - 1]
            found, _ = row_plan(ids, before(d), me, slab, half, x_cells, y_cells)
            rows_v[d] = found
        row_copy().start()

    first = step * chunk
    for u in range(chunk):
        wide = w_ref[u]
        twice[pl.ds(u * y_cells, y_cells), :] = jnp.concatenate([wide, wide], axis=0).T

    def group(g, carry):
        x0 = first + g * GROUP
        for p in range(pairs):
            easts = []
            for u in range(GROUP):
                x = (me * x_local + x0 + u).astype(jnp.float32) + 0.5
                e = x - two(p, lambda s: place[s, 0] * x_cells)
                easts.append(e * e)

            def emit(level, run, values):
                if level is None:
                    start, stride = 0, 1
                else:
                    stride = runs >> level
                    start = (y_cells >> level) + run
                out = tree(values)
                for h in range(GROUP):
                    if h == 0:
                        xrow = x0 // GROUP
                    else:
                        m = 1 << log2(h)
                        xrow = x_local * m // GROUP + (x0 * m // GROUP) + (h - m)
                    at = p * plane + xrow * y_cells + start
                    if stride == 1:
                        field[pl.ds(at, 8), :] = out[h]
                    else:
                        field[pl.ds(at, 8, stride=stride), :] = out[h]

            stack = []
            for r in range(runs):
                t = table[p, r]
                values = []
                for u in range(GROUP):
                    inv = lax.rsqrt(t + easts[u])
                    w = twice[pl.ds((g * GROUP + u) * y_cells + r, 8, stride=runs), :]
                    values.append((w * inv) * (inv * inv))
                level, run = 0, r
                while stack and stack[-1][0] == level:
                    _, other = stack.pop()
                    level, run = level + 1, run >> 1
                    emit(level, run, [o - v for o, v in zip(other, values)])
                    values = [o + v for o, v in zip(other, values)]
                stack.append((level, values))
            emit(None, 0, stack[0][1])
        return carry

    lax.fori_loop(0, chunk // GROUP, group, 0)

    @pl.when(step == last)
    def _():
        coarse = x_local // GROUP

        def finish_x(tile, carry):
            for p in range(pairs):
                at = [p * plane + x * y_cells + tile * 8 for x in range(coarse)]
                values = tree([field[pl.ds(pl.multiple_of(a, 8), 8), :] for a in at])
                for a, v in zip(at, values):
                    field[pl.ds(pl.multiple_of(a, 8), 8), :] = v
            return carry

        lax.fori_loop(0, runs, finish_x, 0)

        def finish_y(block, carry):
            for p in range(pairs):
                at = p * plane + block * (8 * y_cells)
                values = tree([field[pl.ds(at + i, 8, stride=y_cells), :] for i in range(8)])
                for i in range(8):
                    field[pl.ds(at + i, 8, stride=y_cells), :] = values[i]
            return carry

        lax.fori_loop(0, x_local // 8, finish_y, 0)
        even, odd = z_matrix(z_cells, 0), z_matrix(z_cells, 1)
        eye = lax.broadcasted_iota(jnp.int32, (keep, keep), 0) == lax.broadcasted_iota(
            jnp.int32, (keep, keep), 1
        )
        side = lax.broadcasted_iota(jnp.int32, (1, lanes), 1) < z_cells
        row_copy().wait()

        def part(d, ids):
            for s in range(stations):
                for i in range(keep):
                    k = s * keep + i
                    at = (s // 2) * plane + rows_s[d, s, i]
                    taken[2 * k : 2 * k + 2, :] = field[pl.ds(at, 2), :]
            _, factor = row_plan(ids, before(d), me, slab, half, x_cells, y_cells)
            scales = []
            for s in range(stations):
                z_part = kernel_scale * depths[s // 2][0:1, :]
                z_part = jnp.where(side if s % 2 == 0 else jnp.logical_not(side), z_part, 0.0)
                column = jnp.sum(jnp.where(eye, factor[s : s + 1, :], 0.0), axis=1, keepdims=True)
                scales.append(column * z_part)
            scale = jnp.concatenate(scales, axis=0)
            x_even = taken[pl.ds(0, per_row, stride=2), :] * scale
            x_odd = taken[pl.ds(1, per_row, stride=2), :] * scale
            return jnp.dot(
                x_even, even, precision=lax.Precision.HIGHEST, preferred_element_type=jnp.float32
            ) + jnp.dot(x_odd, odd, precision=lax.Precision.HIGHEST, preferred_element_type=jnp.float32)

        def send_part(d, carry):
            parts[d] = part(d, others[d - 1])
            part_copy(d).start()
            return carry

        lax.fori_loop(1, slab, send_part, 0)
        total = part(0, kept[0])
        for d in range(1, slab):
            part_copy(d).wait()
            total = total + arrived[d - 1]
        packed[...] = jnp.dot(
            select[...], total, precision=lax.Precision.HIGHEST, preferred_element_type=jnp.float32
        ).reshape(packed.shape)
        for d in range(1, owners):
            out_copy(d).start()
        own = pltpu.make_async_copy(packed.at[q], out.at[q], own_sem)
        own.start()
        own.wait()
        for d in range(1, owners):
            out_copy(d).wait()


def local(station_place, station_height, cell_weight, kept, dest):
    slab = lax.axis_size("slab")
    owners = lax.axis_size("sta")
    x_local, y_cells, z_cells = cell_weight.shape
    stations = station_place.shape[0]
    keep = kept.shape[2]
    lanes = 2 * z_cells
    per_row = stations * keep
    capacity = max(2, 3 * per_row // owners)
    chunk = 8
    sizes = (slab, owners, stations, keep, x_local, y_cells, z_cells, chunk, capacity)
    pairs = stations // 2
    dma = pltpu.SemaphoreType.DMA
    out = pl.pallas_call(
        functools.partial(whole_kernel, sizes),
        grid=(x_local // chunk,),
        out_shape=jax.ShapeDtypeStruct((owners, capacity, lanes), jnp.float32),
        in_specs=[
            pl.BlockSpec(memory_space=pltpu.SMEM),
            pl.BlockSpec(memory_space=pltpu.SMEM),
            pl.BlockSpec((chunk, z_cells, y_cells), lambda i: (i, 0, 0)),
            pl.BlockSpec(memory_space=pltpu.VMEM),
            pl.BlockSpec(memory_space=pltpu.VMEM),
        ],
        out_specs=pl.BlockSpec(memory_space=pl.ANY),
        scratch_shapes=[
            pltpu.VMEM((pairs * x_local * y_cells, lanes), jnp.float32),
            pltpu.VMEM((chunk * y_cells, lanes), jnp.float32),
            pltpu.VMEM((pairs, y_cells // 8, 8, lanes), jnp.float32),
            pltpu.VMEM((owners * capacity, per_row), jnp.float32),
            pltpu.VMEM((slab - 1, stations, keep), jnp.int32),
            pltpu.VMEM((slab, stations, keep), jnp.int32),
            pltpu.SMEM((slab, stations, keep), jnp.int32),
            pltpu.VMEM((2 * per_row, lanes), jnp.float32),
            pltpu.VMEM((slab, per_row, lanes), jnp.float32),
            pltpu.VMEM((slab - 1, per_row, lanes), jnp.float32),
            pltpu.VMEM((owners, capacity, lanes), jnp.float32),
            dma,
            dma((slab - 1,)),
            dma((slab - 1,)),
            dma((slab - 1,)),
            dma((slab - 1,)),
            dma((owners - 1,)),
            dma((owners - 1,)),
            dma,
        ],
        compiler_params=pltpu.CompilerParams(
            collective_id=0, has_side_effects=True, vmem_limit_bytes=60 * 1024 * 1024
        ),
    )(
        station_place,
        station_height,
        jnp.transpose(cell_weight, (0, 2, 1)),
        kept,
        jnp.transpose(dest, (0, 1, 3, 2)).reshape(stations, 1, keep),
    )
    return out.reshape(1, 1, owners, capacity, lanes)


def solution(mesh):
    placed = (
        P("sta", None),
        P("sta"),
        P("slab", None, None),
        P("slab", "sta", None),
        P("slab", "sta", None, None),
    )
    return jax.shard_map(
        local,
        mesh=mesh,
        in_specs=placed,
        out_specs=P("slab", "sta", None, None, None),
        check_vma=False,
    )
```

time: 56.1 us -> 37.6 us (0.67)
  blocking collectives: 9.56 us -> 0 us
  local copies, waits for them, and re-layouts: 10.4 us -> 2.88 us
  other arithmetic: 0.66 us -> 0 us
  Pallas kernels: 35.1 us -> 34.5 us
    all_gather x1 -> x0, blocking collectives: 9.56 us -> none  [local(): lax.all_gather(kept, 'slab', axis=0, tiled=True).reshape(slab, per_row)]
    unnamed x14 -> x2, local copies, waits for them, and re-layouts: 9.75 us -> 2.88 us
    reshape x2 -> x0, local copies, waits for them, and re-layouts: 0.68 us -> none  [the longest x1 0.6 us: local(): dest.reshape(1, per_row)]
    unnamed x1 -> x0, other arithmetic: 0.66 us -> none
    pallas_call x2 -> x1, Pallas kernels: 35.1 us -> 34.5 us  [local(): pl.pallas_call(functools.partial(whole_kernel, sizes), grid=(x_local // c...]
where the time goes in v2:
time: 37.6 us; the launch traced here: 37.4 us
  Pallas kernels  34.5 us (92%)
  local copies, waits for them, and re-layouts  2.88 us (8%)
    pallas_call x1, Pallas kernels, local(): pl.pallas_call(functools.partial(whole_kernel, sizes), grid=(x_local // c...  34.5 us
    unnamed x2, local copies, waits for them, and re-layouts  2.88 us

profile of v2, /device:TPU:0, one launch (start us, length us, event | category | flops | bytes accessed | tf_op | source)
XLA Modules:
  0.0 37.4 jit_solution(17754419604737102245)
XLA Ops:
  0.0 1.3 %copy.6.place = f32[4,2]{1,0:T(4,128)} copy(f32[4,2]{0,1:T(2,128)} %param.5) | data formatting | bytes 64 | tf_op args[0]
  1.3 34.5 %shard_map.55 = f32[8,24,128]{2,1,0:T(8,128)} custom-call(f32[4,2]{1,0:T(4,128)} %copy.6.place, f32[4]{0:T(128)} %height.1, f32[64,64,256]{2,1,0:T(8,128)} %bitcast.5, s32[1,4,16]{2,1,0:T(4,128)} %kept.1, s32[4,1,16]{2,1,0:T(1,128)} %bitcast.7), custom_call_target="tpu_custom_call" | custom-call | tf_op jit(solution)/shard_map/pallas_call | solution.py:331
  35.9 1.5 %copy.9 = f32[1,1,8,24,128]{4,3,2,1,0:T(8,128)} copy(f32[1,1,8,24,128]{4,3,2,1,0:T(8,128)} %bitcast.6) | data formatting | bytes 196608
